TPU v7x, 32 devices: a whole 2x2x4 slice. The times are simulated.
32 devices in a mesh: dom: 8 (over y, x, core), feat: 4 (over z).
Axes of the slice: x: 2, y: 2, z: 4, core: 2. Of those that a mesh axis runs over, the one named last changes fastest.
Arguments:
- features: bfloat16 [128, 131072], P('feat', 'dom'), may hold values from -6 to 6
- seed_rows: int32 [2048], P('dom'), may hold values from 0 to 16383
- want_rows: int32 [8, 8, 128], P('dom'), may hold values from 0 to 16383
- live_counts: int32 [8, 8], P('dom'), may hold values from 1 to 128, as said below
- hop_one: int32 [15, 2048], P(None, 'dom'), may hold values from 0 to 1023, as said below
- hop_two: int32 [10, 15, 2048], P(None, None, 'dom'), may hold values from 0 to 1023, as said below
- w1_self: bfloat16 [256, 128], replicated, may hold values from -0.5 to 0.5
- w1_neigh: bfloat16 [256, 128], replicated, may hold values from -0.5 to 0.5
- b1: float32 [256], P('feat'), may hold values from -4 to 4
- w2_self: bfloat16 [256, 256], P(None, 'feat'), may hold values from -0.375 to 0.375
- w2_neigh: bfloat16 [256, 256], P(None, 'feat'), may hold values from -0.375 to 0.375
- b2: float32 [256], P('feat'), may hold values from -4 to 4
Outputs:
- embed: float32 [256, 2048], P('feat', 'dom')
Inputs may be any that keep to these rules, and one draw needn't show every extreme that they name: `want_rows`: slots at or beyond live_counts[r, o] are ignored. `live_counts`: in every draw a quarter of the owners, every fourth one from a drawn offset, receive all 128 slots from every requester. `hop_one`: each entry is o * 128 + c, a position in the buffer of the requester that holds seed s, with c < live_counts of that requester and owner o. `hop_two`: each entry is o * 128 + c, a position in the buffer of the requester that holds seed s, with c < live_counts of that requester and owner o.
All inputs are finite; a program needn't handle non-finite values.
Results may differ from a plain program's by a relative error of at most 0.00036.
Values may be sent and summed in bfloat16 or wider, within the bound.
A program may use at most 64 MiB of HBM per device.

v0:
```python
import jax
import jax.numpy as jnp
from jax import lax
from jax.sharding import PartitionSpec as P

OUT = 256
FAN1 = 15
FAN2 = 10
CAP = 128


def aggregate_counts(fetched, hop_one, hop_two):
    feat_dev, slots = fetched.shape
    width = CAP * 4
    first = hop_one.reshape(1, -1)
    second = hop_two.reshape(FAN2, -1)
    columns = first.shape[1]

    def add_block(blocks, carry):
        start = blocks * width
        piece = lax.dynamic_slice_in_dim(fetched, start, width, 1)
        place = start + lax.broadcasted_iota(jnp.int32, (width, 1), 0)
        pick_one = (first == place).astype(jnp.bfloat16)
        pick_two = jnp.zeros((width, columns), jnp.bfloat16)
        for sample in range(FAN2):
            pick_two = pick_two + (second[sample : sample + 1] == place).astype(jnp.bfloat16)
        own_sum = carry[0] + jnp.dot(piece, pick_one, preferred_element_type=jnp.float32)
        mean_sum = carry[1] + jnp.dot(piece, pick_two, preferred_element_type=jnp.float32)
        return (own_sum, mean_sum)

    zeros = jnp.zeros((feat_dev, columns), jnp.float32)
    own_sum, mean_sum = lax.fori_loop(0, slots // width, add_block, (zeros, zeros))
    return (own_sum.astype(jnp.bfloat16), (mean_sum * (1.0 / FAN2)).astype(jnp.bfloat16))


def per_device(
    features,
    seed_rows,
    want_rows,
    live_counts,
    hop_one,
    hop_two,
    w1_self,
    w1_neigh,
    b1,
    w2_self,
    w2_neigh,
    b2,
):
    feat_dev = features.shape[0]
    seed_dev = seed_rows.shape[0]
    hid_dev = b1.shape[0]
    served = jnp.take(
        features,
        lax.all_to_all(want_rows, "dom", split_axis=1, concat_axis=0, tiled=True)[:, 0, :],
        axis=1,
    )
    returned = lax.all_to_all(served, "dom", split_axis=1, concat_axis=1, tiled=True)
    slot_ids = lax.broadcasted_iota(jnp.int32, (1, returned.shape[2]), 1)
    live_slots = slot_ids < live_counts[0][:, None]
    fetched = jnp.where(live_slots[None], returned, jnp.zeros((), jnp.bfloat16)).reshape(
        feat_dev, -1
    )
    x_one, m_two = aggregate_counts(fetched, hop_one, hop_two)
    x_seed = jnp.take(features, seed_rows, axis=1)
    m_one = jnp.sum(x_one.reshape(feat_dev, FAN1, seed_dev), axis=1, dtype=jnp.float32)
    m_one = (m_one * (1.0 / FAN1)).astype(jnp.bfloat16)
    selves = jnp.concatenate([x_one, x_seed], axis=1)
    means = jnp.concatenate([m_two, m_one], axis=1)
    hid_start = lax.axis_index("feat") * hid_dev
    self_rows = lax.dynamic_slice_in_dim(w1_self, hid_start, hid_dev, 0)
    neigh_rows = lax.dynamic_slice_in_dim(w1_neigh, hid_start, hid_dev, 0)
    self_part = self_rows
    neigh_part = neigh_rows
    total = jnp.dot(
        self_part,
        lax.all_gather(selves, "feat", axis=0, tiled=True),
        preferred_element_type=jnp.float32,
    )
    pre = total + jnp.dot(
        neigh_part,
        lax.all_gather(means, "feat", axis=0, tiled=True),
        preferred_element_type=jnp.float32,
    )
    hidden = jnp.maximum(pre + b1[:, None], 0.0)
    hop_cols = FAN1 * seed_dev
    h_one = hidden[:, :hop_cols]
    h_seed = hidden[:, hop_cols:]
    g_mean = jnp.sum(h_one.reshape(hid_dev, FAN1, seed_dev), axis=1) * (1.0 / FAN1)
    second_self = w2_self.astype(jnp.float32)
    second_neigh = w2_neigh.astype(jnp.float32)
    self_part = second_self
    neigh_part = second_neigh
    total = jnp.dot(
        self_part, h_seed, precision=lax.Precision.HIGHEST, preferred_element_type=jnp.float32
    )
    z_out = (
        lax.psum_scatter(
            total
            + jnp.dot(
                neigh_part,
                g_mean,
                precision=lax.Precision.HIGHEST,
                preferred_element_type=jnp.float32,
            ),
            "feat",
            scatter_dimension=0,
            tiled=True,
        )
        + b2[:, None]
    )
    square = lax.psum(jnp.sum(z_out * z_out, axis=0), "feat")
    return z_out * lax.rsqrt(square * (1.0 / OUT) + 1.0)


def solution(mesh):
    return jax.shard_map(
        per_device,
        mesh=mesh,
        in_specs=(
            P("feat", "dom"),
            P("dom"),
            P("dom", None, None),
            P("dom", None),
            P(None, "dom"),
            P(None, None, "dom"),
            P(),
            P(),
            P("feat"),
            P(None, "feat"),
            P(None, "feat"),
            P("feat"),
        ),
        out_specs=P("feat", "dom"),
        check_vma=False,
    )
```

profile of v0, /device:TPU:0, one launch (start us, length us, event | category | flops | bytes accessed | tf_op | source)
XLA Modules:
  0.0 154.3 jit_solution(16646595926999399263)
XLA Ops:
  6.5 5.3 %all-to-all-start = ((s32[1,8,128]{2,0,1:T(1,128)}), s32[1,8,128]{2,0,1:T(1,128)S(1)}, u32[]{:S(2)}, u32[]{:S(2)}) async-start(s32[1,8,128]{2,0,1:T(1,128)} %bitcast.38), calls=%async_computation | async-start | bytes 8192 | tf_op jit(solution)/shard_map/all_to_all | solution.py:55
  11.9 0.7 compare_select_fusion.2
  12.6 0.7 compare_and_fusion.1
  13.2 4.6 %copy.30 = bf16[32,16384]{0,1:T(8,128)(2,1)} copy(bf16[32,16384]{1,0:T(8,128)(2,1)} %param.14) | data formatting | bytes 2097152 | tf_op args[0]
  17.8 3.5 %gather_fusion.1 = bf16[256,32]{1,0:T(8,128)(2,1)S(1)} fusion(bf16[32,16384]{0,1:T(8,128)(2,1)} %copy.30, s32[1024]{0:T(1024)S(1)} %pad_clamp_fusion), kind=kCustom, calls=%fused_computation.1 | custom fusion | bytes 33792 | tf_op jit(solution)/shard_map/jit(_take)/gather | solution.py:65
  21.3 0.1 select_bitcast_fusion
  21.4 5.6 %gather_fusion = bf16[1024,32]{1,0:T(8,128)(2,1)S(1)} fusion(bf16[32,16384]{0,1:T(8,128)(2,1)} %copy.30, s32[1024]{0:T(1024)S(1)} %fusion.43), kind=kCustom, calls=%fused_computation | custom fusion | bytes 135168 | tf_op jit(solution)/shard_map/jit(_take)/gather | solution.py:53
  27.0 0.1 copy.31
  27.2 0.6 select_bitcast_fusion.1
  27.8 4.2 %all-to-all-start.1 = ((bf16[32,8,128]{2,0,1:T(8,128)(2,1)}), bf16[32,8,128]{2,0,1:T(8,128)(2,1)S(1)}, u32[]{:S(2)}, u32[]{:S(2)}) async-start(bf16[32,8,128]{2,0,1:T(8,128)(2,1)} %select_bitcast_fusion.1), calls=%async_computation.1 | async-start | bytes 131072 | tf_op jit(solution)/shard_map/all_to_all | solution.py:58
  32.0 0.2 all-gather.3.cloned.1.call-start
  32.3 0.1 iota_compare_fusion
  32.3 0.1 copy.34
  32.5 0.1 copy.40
  32.6 4.4 %all-to-all-done.1 = bf16[32,8,128]{2,0,1:T(8,128)(2,1)S(1)} async-done(((bf16[32,8,128]{2,0,1:T(8,128)(2,1)}), bf16[32,8,128]{2,0,1:T(8,128)(2,1)S(1)}, u32[]{:S(2)}, u32[]{:S(2)}) %all-to-all-start.1) | async-done | bytes 65568 | tf_op jit(solution)/shard_map/all_to_all | solution.py:58
  37.1 19.3 %while.16 = (s32[]{:T(128)}, f32[32,3840]{1,0:T(8,128)S(1)}, f32[32,3840]{1,0:T(8,128)S(1)}, bf16[32,1024]{1,0:T(8,128)(2,1)S(1)}, s32[1,3840]{1,0:T(1,128)S(1)}...) while((s32[]{:T(128)}, f32[32,3840]{1,0:T(8,128)S(1)}, ...), condition=%wide.region_1.2_spmd.clone, body=%wide.region_0.1_spmd.clone.sunk | while | flops 311132672 | bytes 2556086 | solution.py:32
  37.1 1.5 fusion.60
  38.6 0.4 slice_reduce_fusion.11
  39.0 7.7 %convolution_add_fusion.4 = f32[32,3840]{1,0:T(8,128)S(1)} fusion(s32[3840]{0:T(1024)S(1)} %get-tuple-element.207, s32[3840]{0:T(1024)S(1)} %get-tuple-element.208, s32[3840]{0:T(1024)S(1)} %get-tuple-element.209, s32[3840]{0:T(1024)S(1)} %get-tuple-element.210, s32[3840]{0:T(1024)S(1)} %get-tuple-element.211, s32[3840]{0:T(1024)S(1)} %get-tuple-element.212, ...), kind=kOutput, calls=%fused_computation.14.clone.1 | convolution fusion | flops 183091200 | bytes 1181701 | tf_op jit(solution)/shard_map/while/body/eval_jaxpr/dot_general | solution.py:28
  46.8 1.5 fusion.60
  48.3 0.4 slice_reduce_fusion.11
  48.7 7.7 %convolution_add_fusion.4 = f32[32,3840]{1,0:T(8,128)S(1)} fusion(s32[3840]{0:T(1024)S(1)} %get-tuple-element.207, s32[3840]{0:T(1024)S(1)} %get-tuple-element.208, s32[3840]{0:T(1024)S(1)} %get-tuple-element.209, s32[3840]{0:T(1024)S(1)} %get-tuple-element.210, s32[3840]{0:T(1024)S(1)} %get-tuple-element.211, s32[3840]{0:T(1024)S(1)} %get-tuple-element.212, ...), kind=kOutput, calls=%fused_computation.14.clone.1 | convolution fusion | flops 183091200 | bytes 1181701 | tf_op jit(solution)/shard_map/while/body/eval_jaxpr/dot_general | solution.py:28
  56.5 0.2 reshape.90
  56.7 0.7 pad_maximum_fusion
  57.4 0.0 all-gather.3.cloned.1.call-update
  57.4 0.0 all-gather.5.cloned.1.call-start
  57.5 0.1 reduce_sum.27
  57.6 0.0 copy-start.3
  57.7 0.7 pad_maximum_fusion.1
  58.4 0.0 all-gather.5.cloned.1.call-update
  58.4 0.0 reduce-scatter.4.cloned.1.call-start
  58.5 26.5 %all-gather.3.cloned.1.call-done = bf16[128,4096]{1,0:T(8,128)(2,1)} async-done(((bf16[32,4096]{1,0:T(8,128)(2,1)}), bf16[128,4096]{1,0:T(8,128)(2,1)}) %all-gather.3.cloned.1.call-update) | async-done | bytes 1048592 | tf_op jit(solution)/shard_map/all_gather | solution.py:77
  84.9 1.5 fusion.40
  86.5 27.4 %all-gather.5.cloned.1.call-done = bf16[128,4096]{1,0:T(8,128)(2,1)} async-done(((bf16[32,4096]{1,0:T(8,128)(2,1)}), bf16[128,4096]{1,0:T(8,128)(2,1)}) %all-gather.5.cloned.1.call-update) | async-done | bytes 1048592 | tf_op jit(solution)/shard_map/all_gather | solution.py:82
  113.9 1.5 fusion.33
  115.4 0.1 slice.93
  115.5 0.3 fusion.35
  115.9 0.3 reshape.89
  116.2 0.2 reduce_sum.28
  116.4 0.3 fusion.34
  116.7 0.8 copy.36
  117.5 0.0 reduce-scatter.4.cloned.1.call-update
  117.5 19.5 %reduce-scatter.4.cloned.1.call-done = f32[64,256]{1,0:T(8,128)} async-done(((f32[256,256]{1,0:T(8,128)}), f32[64,256]{1,0:T(8,128)}) %reduce-scatter.4.cloned.1.call-update) | async-done | bytes 65552
  137.1 0.9 copy.37
  138.0 0.1 multiply_reduce_fusion
  138.1 8.8 %psum.7 = f32[256]{0:T(256)S(1)} all-reduce(f32[256]{0:T(256)S(1)} %multiply_reduce_fusion), channel_id=1, replica_groups=mesh['dom'=8,'feat'=4] {'feat'}, use_global_device_ids=true, to_apply=%region_6.7 | all-reduce | flops 256 | bytes 2048 | tf_op jit(solution)/shard_map/psum | solution.py:112
  147.0 0.1 add_multiply_fusion
  147.1 0.7 copy.35
  (32 shorter events, 0.3 us)
Async XLA Ops:
  6.5 78.4 %copy-start = (bf16[256,128]{1,0:T(8,128)(2,1)S(1)}, bf16[256,128]{1,0:T(8,128)(2,1)}, u32[]{:S(2)}) copy-start(bf16[256,128]{1,0:T(8,128)(2,1)} %param.20) | copy-start | bytes 196612
  6.5 25.7 %copy-start.7 = (s32[1,8]{1,0:T(1,128)S(1)}, s32[1,8]{1,0:T(1,128)}, u32[]{:S(2)}) copy-start(s32[1,8]{1,0:T(1,128)} %param.17) | copy-start | bytes 100
  6.5 25.9 %copy-start.4 = (s32[15,256]{1,0:T(8,128)S(1)}, s32[15,256]{1,0:T(8,128)}, u32[]{:S(2)}) copy-start(s32[15,256]{1,0:T(8,128)} %param.18) | copy-start | bytes 46084
  6.5 25.9 %copy-start.1 = (s32[10,15,256]{2,1,0:T(8,128)S(1)}, s32[10,15,256]{2,1,0:T(8,128)}, u32[]{:S(2)}) copy-start(s32[10,15,256]{2,1,0:T(8,128)} %param.19) | copy-start | bytes 460804
  6.5 14.9 %all-to-all-start = ((s32[1,8,128]{2,0,1:T(1,128)}), s32[1,8,128]{2,0,1:T(1,128)S(1)}, u32[]{:S(2)}, u32[]{:S(2)}) async-start(s32[1,8,128]{2,0,1:T(1,128)} %bitcast.38), calls=%async_computation | async-start | bytes 8192 | tf_op jit(solution)/shard_map/all_to_all | solution.py:55
  27.8 9.2 %all-to-all-start.1 = ((bf16[32,8,128]{2,0,1:T(8,128)(2,1)}), bf16[32,8,128]{2,0,1:T(8,128)(2,1)S(1)}, u32[]{:S(2)}, u32[]{:S(2)}) async-start(bf16[32,8,128]{2,0,1:T(8,128)(2,1)} %select_bitcast_fusion.1), calls=%async_computation.1 | async-start | bytes 131072 | tf_op jit(solution)/shard_map/all_to_all | solution.py:58
  32.0 52.9 %all-gather.3.cloned.1.call-start = ((), (), s32[]{:S(2)}) async-start(), calls=%async_computation.3 | async-start | bytes 1310720 | tf_op jit(solution)/shard_map/all_gather | solution.py:77
  56.4 57.5 %copy-start.6 = (f32[64]{0:T(128)S(1)}, f32[64]{0:T(128)}, u32[]{:S(2)}) copy-start(f32[64]{0:T(128)} %param.22) | copy-start | bytes 772
  57.4 56.5 %all-gather.5.cloned.1.call-start = ((), (), s32[]{:S(2)}) async-start(), calls=%async_computation.4 | async-start | bytes 1310720 | tf_op jit(solution)/shard_map/all_gather | solution.py:82
  57.6 57.9 %copy-start.3 = (bf16[256,64]{0,1:T(8,128)(2,1)S(1)}, bf16[256,64]{0,1:T(8,128)(2,1)}, u32[]{:S(2)}) copy-start(bf16[256,64]{0,1:T(8,128)(2,1)} %param.23) | copy-start | bytes 98308
  58.4 78.7 %reduce-scatter.4.cloned.1.call-start = ((), (), s32[]{:S(2)}) async-start(), calls=%async_computation.5 | async-start | bytes 327680
  86.4 29.9 %copy-start.2 = (bf16[256,64]{0,1:T(8,128)(2,1)S(1)}, bf16[256,64]{0,1:T(8,128)(2,1)}, u32[]{:S(2)}) copy-start(bf16[256,64]{0,1:T(8,128)(2,1)} %param.24) | copy-start | bytes 98308
  115.4 22.6 %copy-start.5 = (f32[64]{0:T(128)S(1)}, f32[64]{0:T(128)}, u32[]{:S(2)}) copy-start(f32[64]{0:T(128)} %param.25) | copy-start | bytes 772
Sparse Core Ops, SparseCore 0:
  57.5 27.3 all-gather.2
  86.5 27.3 all-gather.4
  117.7 19.3 reduce-scatter.3
where the time goes:
time: 155 us; the launch traced here: 154 us
  waiting for transfers between devices  77.9 us (50%)
  matrix products  22 us (14%)
  local copies, waits for them, and re-layouts  17.9 us (12%)
  between operations  13.4 us (9%)
  starting transfers between devices  9.84 us (6%)
  blocking collectives  8.85 us (6%)
  other arithmetic  4.35 us (3%)
    all_gather x1, waiting for transfers between devices, per_device(): lax.all_gather(means, 'feat', axis=0, tiled=True)  27.4 us
    all_gather x1, waiting for transfers between devices, per_device(): lax.all_gather(selves, 'feat', axis=0, tiled=True)  26.5 us
    unnamed x4, waiting for transfers between devices  19.6 us
    dot_general x2, matrix products, add_block(): jnp.dot(piece, pick_two, preferred_element_type=jnp.float32)  15.4 us
    psum x1, blocking collectives, per_device(): square = lax.psum(jnp.sum(z_out * z_out, axis=0), 'feat')  8.85 us
    unnamed x22, local copies, waits for them, and re-layouts  6.56 us
    gather x2, local copies, waits for them, and re-layouts, per_device(): jnp.take(features, lax.all_to_all(want_rows, 'dom', split_axis=1, concat_...  5.73 us
    all_to_all x1, starting transfers between devices, per_device(): lax.all_to_all(want_rows, 'dom', split_axis=1, concat_axis=0, tiled=True)  5.34 us
  transfers between devices with their start and end apart: 5, of which 4 were waited for; matrix products, arithmetic and copies ran while one was open for 8% of the time, Pallas kernels for 0%

commit v1 on v0

--- a/solution.py
+++ b/solution.py
@@ -7,6 +7,16 @@
 FAN1 = 15
 FAN2 = 10
 CAP = 128
+
+
+def ring_gather(x, axis, dim):
+    ways, here, turn = (lax.axis_size(axis), lax.axis_index(axis), x.shape[dim])
+    dims = [n * ways if d == dim else n for d, n in enumerate(x.shape)]
+    full = lax.dynamic_update_slice_in_dim(jnp.zeros(dims, x.dtype), x, here * turn, axis=dim)
+    for far in range(1, ways):
+        x = lax.ppermute(x, axis, [(d, (d + 1) % ways) for d in range(ways)])
+        full = lax.dynamic_update_slice_in_dim(full, x, (here - far) % ways * turn, axis=dim)
+    return full
 
 
 def aggregate_counts(fetched, hop_one, hop_two):
@@ -78,9 +88,7 @@
         preferred_element_type=jnp.float32,
     )
     pre = total + jnp.dot(
-        neigh_part,
-        lax.all_gather(means, "feat", axis=0, tiled=True),
-        preferred_element_type=jnp.float32,
+        neigh_part, ring_gather(means, "feat", 0), preferred_element_type=jnp.float32
     )
     hidden = jnp.maximum(pre + b1[:, None], 0.0)
     hop_cols = FAN1 * seed_dev

time: 155 us -> 138 us (0.89)
  waiting for transfers between devices: 77.9 us -> 59.2 us
  starting transfers between devices: 9.84 us -> 12.6 us
    ppermute x0 -> x3, waiting for transfers between devices: none -> 37.3 us  [ring_gather(): x = lax.ppermute(x, axis, [(d, (d + 1) % ways) for d in range(ways)])]
    all_gather x1 -> x0, waiting for transfers between devices: 27.4 us -> none  [per_device(): lax.all_gather(means, 'feat', axis=0, tiled=True)]
    all_gather x1, waiting for transfers between devices: 26.5 us -> 0.02 us  [per_device(): lax.all_gather(selves, 'feat', axis=0, tiled=True)]
    ppermute x0 -> x3, starting transfers between devices: none -> 2.81 us  [ring_gather(): x = lax.ppermute(x, axis, [(d, (d + 1) % ways) for d in range(ways)])]
    unnamed x4 -> x3, waiting for transfers between devices: 19.6 us -> 17.5 us
  transfers between devices with their start and end apart: 5 -> 7, of which waited for: 4 -> 5; matrix products, arithmetic and copies ran while one was open for 8% -> 8% of each run, Pallas kernels for 0% -> 0%
where the time goes in v1:
time: 138 us
  waiting for transfers between devices  59.2 us (43%)
  matrix products  21.5 us (16%)
  local copies, waits for them, and re-layouts  18 us (13%)
  between operations  13.8 us (10%)
  starting transfers between devices  12.6 us (9%)
  blocking collectives  8.74 us (6%)
  other arithmetic  3.66 us (3%)
    ppermute x3, waiting for transfers between devices, ring_gather(): x = lax.ppermute(x, axis, [(d, (d + 1) % ways) for d in range(ways)])  37.3 us
    unnamed x3, waiting for transfers between devices  17.5 us
    dot_general x2, matrix products, add_block(): jnp.dot(piece, pick_two, preferred_element_type=jnp.float32)  15.4 us
    psum x1, blocking collectives, per_device(): square = lax.psum(jnp.sum(z_out * z_out, axis=0), 'feat')  8.74 us
    unnamed x22, local copies, waits for them, and re-layouts  6.56 us
    gather x2, local copies, waits for them, and re-layouts, per_device(): jnp.take(features, lax.all_to_all(want_rows, 'dom', split_axis=1, concat_...  5.73 us
    all_to_all x1, starting transfers between devices, per_device(): lax.all_to_all(want_rows, 'dom', split_axis=1, concat_axis=0, tiled=True)  5.34 us
    all_to_all x1, waiting for transfers between devices, per_device(): lax.all_to_all(served, 'dom', split_axis=1, concat_axis=1, tiled=True)  4.4 us
  transfers between devices with their start and end apart: 7, of which 5 were waited for; matrix products, arithmetic and copies ran while one was open for 8% of the time, Pallas kernels for 0%

profile of v1, /device:TPU:0, one launch (start us, length us, event | category | flops | bytes accessed | tf_op | source)
XLA Modules:
  0.0 137.6 jit_solution(2198998284059500569)
XLA Ops:
  6.5 5.3 %all-to-all-start = ((s32[1,8,128]{2,0,1:T(1,128)}), s32[1,8,128]{2,0,1:T(1,128)S(1)}, u32[]{:S(2)}, u32[]{:S(2)}) async-start(s32[1,8,128]{2,0,1:T(1,128)} %bitcast.38), calls=%async_computation | async-start | bytes 8192 | tf_op jit(solution)/shard_map/all_to_all | solution.py:65
  11.9 0.7 compare_select_fusion.2
  12.6 0.7 compare_and_fusion.1
  13.2 4.6 %copy.30 = bf16[32,16384]{0,1:T(8,128)(2,1)} copy(bf16[32,16384]{1,0:T(8,128)(2,1)} %param.14) | data formatting | bytes 2097152 | tf_op args[0]
  17.8 3.5 %gather_fusion.1 = bf16[256,32]{1,0:T(8,128)(2,1)S(1)} fusion(bf16[32,16384]{0,1:T(8,128)(2,1)} %copy.30, s32[1024]{0:T(1024)S(1)} %pad_clamp_fusion), kind=kCustom, calls=%fused_computation.1 | custom fusion | bytes 33792 | tf_op jit(solution)/shard_map/jit(_take)/gather | solution.py:75
  21.3 0.1 select_bitcast_fusion
  21.4 5.6 %gather_fusion = bf16[1024,32]{1,0:T(8,128)(2,1)S(1)} fusion(bf16[32,16384]{0,1:T(8,128)(2,1)} %copy.30, s32[1024]{0:T(1024)S(1)} %fusion.43), kind=kCustom, calls=%fused_computation | custom fusion | bytes 135168 | tf_op jit(solution)/shard_map/jit(_take)/gather | solution.py:63
  27.0 0.1 copy.31
  27.2 0.6 select_bitcast_fusion.1
  27.8 4.2 %all-to-all-start.1 = ((bf16[32,8,128]{2,0,1:T(8,128)(2,1)}), bf16[32,8,128]{2,0,1:T(8,128)(2,1)S(1)}, u32[]{:S(2)}, u32[]{:S(2)}) async-start(bf16[32,8,128]{2,0,1:T(8,128)(2,1)} %select_bitcast_fusion.1), calls=%async_computation.1 | async-start | bytes 131072 | tf_op jit(solution)/shard_map/all_to_all | solution.py:68
  32.0 0.2 all-gather.2.cloned.1.call-start
  32.3 0.1 iota_compare_fusion
  32.3 0.1 copy.34
  32.5 0.1 copy.40
  32.6 4.4 %all-to-all-done.1 = bf16[32,8,128]{2,0,1:T(8,128)(2,1)S(1)} async-done(((bf16[32,8,128]{2,0,1:T(8,128)(2,1)}), bf16[32,8,128]{2,0,1:T(8,128)(2,1)S(1)}, u32[]{:S(2)}, u32[]{:S(2)}) %all-to-all-start.1) | async-done | bytes 65568 | tf_op jit(solution)/shard_map/all_to_all | solution.py:68
  37.1 19.3 %while.16 = (s32[]{:T(128)}, f32[32,3840]{1,0:T(8,128)S(1)}, f32[32,3840]{1,0:T(8,128)S(1)}, bf16[32,1024]{1,0:T(8,128)(2,1)S(1)}, s32[1,3840]{1,0:T(1,128)S(1)}...) while((s32[]{:T(128)}, f32[32,3840]{1,0:T(8,128)S(1)}, ...), condition=%wide.region_1.2_spmd.clone, body=%wide.region_0.1_spmd.clone.sunk | while | flops 311132672 | bytes 2556086 | solution.py:42
  37.1 1.5 %fusion.60 = f32[32,3840]{1,0:T(8,128)S(1)} fusion(s32[3840]{0:T(1024)S(1)} %reduce.24, s32[512]{0:T(512)S(1)} %iota_add_fusion.2, f32[32,3840]{1,0:T(8,128)S(1)} %get-tuple-element.230, pred[]{:T(512)S(6)} %compare.6, bf16[32,1024]{1,0:T(8,128)(2,1)S(1)} %get-tuple-element.242, s32[]{:T(128)S(6)} %select_n.104), kind=kOutput, calls=%fused_computation.15.clone.1 | convolution fusion | flops 128040960 | bytes 1034245 | tf_op jit(solution)/shard_map/while/body/eval_jaxpr/dot_general | solution.py:37
  38.6 0.4 slice_reduce_fusion.11
  39.0 7.7 %convolution_add_fusion.4 = f32[32,3840]{1,0:T(8,128)S(1)} fusion(s32[3840]{0:T(1024)S(1)} %get-tuple-element.209, s32[3840]{0:T(1024)S(1)} %get-tuple-element.210, s32[3840]{0:T(1024)S(1)} %get-tuple-element.211, s32[3840]{0:T(1024)S(1)} %get-tuple-element.212, s32[3840]{0:T(1024)S(1)} %get-tuple-element.213, s32[3840]{0:T(1024)S(1)} %get-tuple-element.214, ...), kind=kOutput, calls=%fused_computation.14.clone.1 | convolution fusion | flops 183091200 | bytes 1181701 | tf_op jit(solution)/shard_map/while/body/eval_jaxpr/dot_general | solution.py:38
  46.8 1.5 %fusion.60 = f32[32,3840]{1,0:T(8,128)S(1)} fusion(s32[3840]{0:T(1024)S(1)} %reduce.24, s32[512]{0:T(512)S(1)} %iota_add_fusion.2, f32[32,3840]{1,0:T(8,128)S(1)} %get-tuple-element.230, pred[]{:T(512)S(6)} %compare.6, bf16[32,1024]{1,0:T(8,128)(2,1)S(1)} %get-tuple-element.242, s32[]{:T(128)S(6)} %select_n.104), kind=kOutput, calls=%fused_computation.15.clone.1 | convolution fusion | flops 128040960 | bytes 1034245 | tf_op jit(solution)/shard_map/while/body/eval_jaxpr/dot_general | solution.py:37
  48.3 0.4 slice_reduce_fusion.11
  48.7 7.7 %convolution_add_fusion.4 = f32[32,3840]{1,0:T(8,128)S(1)} fusion(s32[3840]{0:T(1024)S(1)} %get-tuple-element.209, s32[3840]{0:T(1024)S(1)} %get-tuple-element.210, s32[3840]{0:T(1024)S(1)} %get-tuple-element.211, s32[3840]{0:T(1024)S(1)} %get-tuple-element.212, s32[3840]{0:T(1024)S(1)} %get-tuple-element.213, s32[3840]{0:T(1024)S(1)} %get-tuple-element.214, ...), kind=kOutput, calls=%fused_computation.14.clone.1 | convolution fusion | flops 183091200 | bytes 1181701 | tf_op jit(solution)/shard_map/while/body/eval_jaxpr/dot_general | solution.py:38
  56.4 0.2 reshape.90
  56.7 0.1 reduce_sum.27
  56.8 0.1 broadcast_in_dim.52
  57.0 1.6 %collective-permute-start = (bf16[32,4096]{1,0:T(8,128)(2,1)S(1)}, bf16[32,4096]{1,0:T(8,128)(2,1)S(1)}, u32[]{:S(2)}, u32[]{:S(2)}) collective-permute-start(bf16[32,4096]{1,0:T(8,128)(2,1)S(1)} %get-tuple-element.160), channel_id=1, source_target_pairs={{0,1},{1,2},{2,3},{3,0},{4,5},{5,6},{6,7},{7,4},{8,9},{9,10},{10,1... | collective-permute-start | bytes 786440 | tf_op jit(solution)/shard_map/ppermute | solution.py:17
  58.6 0.7 pad_maximum_fusion
  59.3 0.0 all-gather.2.cloned.1.call-update
  59.4 0.0 reduce-scatter.4.cloned.1.call-start
  59.5 7.3 %collective-permute-done = bf16[32,4096]{1,0:T(8,128)(2,1)S(1)} collective-permute-done((bf16[32,4096]{1,0:T(8,128)(2,1)S(1)}, bf16[32,4096]{1,0:T(8,128)(2,1)S(1)}, u32[]{:S(2)}, u32[]{:S(2)}) %collective-permute-start) | collective-permute-done | bytes 262176 | tf_op jit(solution)/shard_map/ppermute | solution.py:17
  66.8 15.8 %collective-permute-done.1 = bf16[32,4096]{1,0:T(8,128)(2,1)S(1)} collective-permute-done((bf16[32,4096]{1,0:T(8,128)(2,1)S(1)}, bf16[32,4096]{1,0:T(8,128)(2,1)S(1)}, u32[]{:S(2)}, u32[]{:S(2)}) %collective-permute-start.1) | collective-permute-done | bytes 262176 | tf_op jit(solution)/shard_map/ppermute | solution.py:17
  82.6 1.2 collective-permute-start.2
  83.8 14.2 %collective-permute-done.2 = bf16[32,4096]{1,0:T(8,128)(2,1)S(1)} collective-permute-done((bf16[32,4096]{1,0:T(8,128)(2,1)S(1)}, bf16[32,4096]{1,0:T(8,128)(2,1)S(1)}, u32[]{:S(2)}, u32[]{:S(2)}) %collective-permute-start.2) | collective-permute-done | bytes 262176 | tf_op jit(solution)/shard_map/ppermute | solution.py:17
  98.0 0.0 all-gather.2.cloned.1.call-done
  98.1 1.5 %fusion.40 = f32[64,4096]{1,0:T(8,128)S(1)} fusion(bf16[128,4096]{1,0:T(8,128)(2,1)} %all-gather.2.cloned.1.call-done, bf16[256,128]{1,0:T(8,128)(2,1)S(1)} %copy-done, s32[]{:T(128)S(6)} %select_n.71), kind=kOutput, calls=%fused_computation.73 | convolution fusion | flops 67108864 | bytes 2113540 | tf_op jit(solution)/shard_map/dot_general | solution.py:85
  99.6 1.0 fusion.33
  100.7 0.1 slice.93
  100.7 0.3 fusion.35
  101.1 0.3 reshape.89
  101.4 0.2 reduce_sum.28
  101.6 0.3 fusion.34
  101.9 0.8 copy.36
  102.8 17.4 %reduce-scatter.4.cloned.1.call-done = f32[64,256]{1,0:T(8,128)} async-done(((f32[256,256]{1,0:T(8,128)}), f32[64,256]{1,0:T(8,128)}) %reduce-scatter.4.cloned.1.call-update) | async-done | bytes 65552
  120.2 0.9 copy.37
  121.1 0.1 multiply_reduce_fusion
  121.2 8.7 %psum.7 = f32[256]{0:T(256)S(1)} all-reduce(f32[256]{0:T(256)S(1)} %multiply_reduce_fusion), channel_id=1, replica_groups=mesh['dom'=8,'feat'=4] {'feat'}, use_global_device_ids=true, to_apply=%region_6.7 | all-reduce | flops 256 | bytes 2048 | tf_op jit(solution)/shard_map/psum | solution.py:120
  130.0 0.1 add_multiply_fusion
  130.1 0.7 copy.35
  (39 shorter events, 0.4 us)
Async XLA Ops:
  6.5 91.5 %copy-start = (bf16[256,128]{1,0:T(8,128)(2,1)S(1)}, bf16[256,128]{1,0:T(8,128)(2,1)}, u32[]{:S(2)}) copy-start(bf16[256,128]{1,0:T(8,128)(2,1)} %param.20) | copy-start | bytes 196612
  6.5 25.7 %copy-start.7 = (s32[1,8]{1,0:T(1,128)S(1)}, s32[1,8]{1,0:T(1,128)}, u32[]{:S(2)}) copy-start(s32[1,8]{1,0:T(1,128)} %param.17) | copy-start | bytes 100
  6.5 25.9 %copy-start.4 = (s32[15,256]{1,0:T(8,128)S(1)}, s32[15,256]{1,0:T(8,128)}, u32[]{:S(2)}) copy-start(s32[15,256]{1,0:T(8,128)} %param.18) | copy-start | bytes 46084
  6.5 25.9 %copy-start.1 = (s32[10,15,256]{2,1,0:T(8,128)S(1)}, s32[10,15,256]{2,1,0:T(8,128)}, u32[]{:S(2)}) copy-start(s32[10,15,256]{2,1,0:T(8,128)} %param.19) | copy-start | bytes 460804
  6.5 14.9 %all-to-all-start = ((s32[1,8,128]{2,0,1:T(1,128)}), s32[1,8,128]{2,0,1:T(1,128)S(1)}, u32[]{:S(2)}, u32[]{:S(2)}) async-start(s32[1,8,128]{2,0,1:T(1,128)} %bitcast.38), calls=%async_computation | async-start | bytes 8192 | tf_op jit(solution)/shard_map/all_to_all | solution.py:65
  27.8 9.2 %all-to-all-start.1 = ((bf16[32,8,128]{2,0,1:T(8,128)(2,1)}), bf16[32,8,128]{2,0,1:T(8,128)(2,1)S(1)}, u32[]{:S(2)}, u32[]{:S(2)}) async-start(bf16[32,8,128]{2,0,1:T(8,128)(2,1)} %select_bitcast_fusion.1), calls=%async_computation.1 | async-start | bytes 131072 | tf_op jit(solution)/shard_map/all_to_all | solution.py:68
  32.0 66.0 %all-gather.2.cloned.1.call-start = ((), (), s32[]{:S(2)}) async-start(), calls=%async_computation.3 | async-start | bytes 1310720 | tf_op jit(solution)/shard_map/all_gather | solution.py:87
  56.6 43.0 %copy-start.6 = (f32[64]{0:T(128)S(1)}, f32[64]{0:T(128)}, u32[]{:S(2)}) copy-start(f32[64]{0:T(128)} %param.22) | copy-start | bytes 772
  57.0 9.8 %collective-permute-start = (bf16[32,4096]{1,0:T(8,128)(2,1)S(1)}, bf16[32,4096]{1,0:T(8,128)(2,1)S(1)}, u32[]{:S(2)}, u32[]{:S(2)}) collective-permute-start(bf16[32,4096]{1,0:T(8,128)(2,1)S(1)} %get-tuple-element.160), channel_id=1, source_target_pairs={{0,1},{1,2},{2,3},{3,0},{4,5},{5,6},{6,7},{7,4},{8,9},{9,10},{10,1... | collective-permute-start | bytes 786440 | tf_op jit(solution)/shard_map/ppermute | solution.py:17
  59.4 60.8 %reduce-scatter.4.cloned.1.call-start = ((), (), s32[]{:S(2)}) async-start(), calls=%async_computation.4 | async-start | bytes 327680
  66.7 15.8 %collective-permute-start.1 = (bf16[32,4096]{1,0:T(8,128)(2,1)S(1)}, bf16[32,4096]{1,0:T(8,128)(2,1)S(1)}, u32[]{:S(2)}, u32[]{:S(2)}) collective-permute-start(bf16[32,4096]{1,0:T(8,128)(2,1)S(1)} %collective-permute-done), channel_id=1, source_target_pairs={{0,1},{1,2},{2,3},{3,0},{4,5},{5,6},{6,7},{7,4},{8,9},{9,10},{10,1... | collective-permute-start | bytes 786440 | tf_op jit(solution)/shard_map/ppermute | solution.py:17
  82.6 15.4 %collective-permute-start.2 = (bf16[32,4096]{1,0:T(8,128)(2,1)S(1)}, bf16[32,4096]{1,0:T(8,128)(2,1)S(1)}, u32[]{:S(2)}, u32[]{:S(2)}) collective-permute-start(bf16[32,4096]{1,0:T(8,128)(2,1)S(1)} %collective-permute-done.1), channel_id=1, source_target_pairs={{0,1},{1,2},{2,3},{3,0},{4,5},{5,6},{6,7},{7,4},{8,9},{9,10},{10,1... | collective-permute-start | bytes 786440 | tf_op jit(solution)/shard_map/ppermute | solution.py:17
  83.8 17.0 %copy-start.3 = (bf16[256,64]{0,1:T(8,128)(2,1)S(1)}, bf16[256,64]{0,1:T(8,128)(2,1)}, u32[]{:S(2)}) copy-start(bf16[256,64]{0,1:T(8,128)(2,1)} %param.23) | copy-start | bytes 98308
  99.6 2.0 %copy-start.2 = (bf16[256,64]{0,1:T(8,128)(2,1)S(1)}, bf16[256,64]{0,1:T(8,128)(2,1)}, u32[]{:S(2)}) copy-start(bf16[256,64]{0,1:T(8,128)(2,1)} %param.24) | copy-start | bytes 98308
  100.6 20.5 %copy-start.5 = (f32[64]{0:T(128)S(1)}, f32[64]{0:T(128)}, u32[]{:S(2)}) copy-start(f32[64]{0:T(128)} %param.25) | copy-start | bytes 772
Sparse Core Ops, SparseCore 0:
  59.5 35.7 all-gather.1
  102.9 17.2 reduce-scatter.3
